TPU v7x, 256 devices: a whole 4x4x8 slice. The times are simulated.
256 devices in a mesh: bra: 16 (over z_lo, x), ket: 8 (over y, core), mpo: 2 (over z_hi).
Axes of the slice: x: 4, y: 4, z: 8 (z_hi: 2, z_lo: 4; z = z_hi * 4 + z_lo), core: 2. Of those that a mesh axis runs over, the one named last changes fastest.
Arguments:
- left_env: bfloat16 [4, 3072, 3072], P('mpo', 'bra', 'ket'), may hold values from -6 to 6
- site_tensor: bfloat16 [3072, 4, 3072], P('bra', None, 'ket'), may hold values from -0.0546875 to 0.0546875
- block_values: float32 [12, 4, 4], replicated, may hold values from -3 to 3
- pair_in: int32 [12], replicated, may hold values from 0 to 3
- pair_out: int32 [12], replicated, may hold values from 0 to 3, as said below
Outputs:
- new_env: bfloat16 [4, 3072, 3072], P('mpo', 'bra', 'ket')
Inputs may be any that keep to these rules, and one draw needn't show every extreme that they name: `pair_out`: every component number 0 to 3 appears at least once.
All inputs are finite; a program needn't handle non-finite values.
Results may differ from a plain program's by a relative error of at most 0.018.
Values may be sent and summed in bfloat16 or wider, within the bound.
No kernel may reach another device: no remote copies, remote signals or barrier semaphores. Data moves between devices by JAX's collectives and lax.ppermute only.
A program may use at most 64 MiB of HBM per device.

v0:
```python
import jax
import jax.numpy as jnp
from jax import lax
from jax.sharding import Mesh
from jax.sharding import PartitionSpec as P

K = 4
BRA = ("bra_0", "bra_1")


def from_everyone(value, axis):
    copies = jnp.broadcast_to(value, (lax.axis_size(axis), *value.shape))
    return lax.all_to_all(copies, axis, split_axis=0, concat_axis=0, tiled=True)


def joined_along(blocks, dim):
    blocks = jnp.moveaxis(blocks, 0, dim)
    dims = blocks.shape
    return blocks.reshape(*dims[:dim], dims[dim] * dims[dim + 1], *dims[dim + 2 :])


def gathered_copies(value, axis, dim):
    blocks = from_everyone(value, axis)
    return joined_along(blocks, dim)


def reduced_to_own(blocks, axes, sequence):
    dims = [lax.axis_size(a) for a in axes]
    blocks = blocks.reshape(*dims, *blocks.shape[1:])
    blocks = blocks.transpose(*sequence, *range(len(axes), blocks.ndim))
    blocks = blocks.reshape(-1, *blocks.shape[len(axes) :])
    for k in sequence:
        blocks = lax.psum_scatter(blocks, axes[k], scatter_dimension=0, tiled=True)
    return blocks[0]


def cut_along(value, dim, peers):
    dims = value.shape
    blocks = value.reshape(*dims[:dim], peers, dims[dim] // peers, *dims[dim + 1 :])
    return jnp.moveaxis(blocks, dim, 0)


def scatter_axes(value, axes, sequence, dim):
    peers = lax.axis_size(axes)
    return reduced_to_own(cut_along(value, dim, peers), axes, sequence)


def local(left_env, site_tensor, block_values, pair_in, pair_out):
    comps_loc = left_env.shape[0]
    rows_loc = left_env.shape[1]
    cols_loc = left_env.shape[2]
    phys = site_tensor.shape[1]
    comps = jnp.arange(K, dtype=jnp.int32)
    hot_out = (pair_out[:, None] == comps[None, :]).astype(jnp.float32)
    hot_in = (pair_in[:, None] == comps[None, :]).astype(jnp.float32)
    mixing = jnp.einsum("pv,pw,pst->vswt", hot_out, hot_in, block_values)
    own_start = lax.axis_index("mpo") * comps_loc
    site_full = lax.all_gather(site_tensor, BRA, axis=0, tiled=True)
    full_rows = site_full.shape[0]
    site_flat = site_full.reshape(full_rows, phys * cols_loc)
    piece = gathered_copies(left_env, "ket", 2)
    width = piece.shape[2]
    panel = site_flat
    half = jnp.dot(
        piece.reshape(comps_loc * rows_loc, width), panel, preferred_element_type=jnp.float32
    )
    half = half.astype(jnp.bfloat16).reshape(comps_loc, rows_loc, phys, cols_loc)
    halves = gathered_copies(half, "mpo", 0)
    mix_rows = lax.dynamic_slice_in_dim(mixing, own_start, comps_loc, 0)
    mixed = jnp.einsum("vswt,watc->vasc", mix_rows, halves.astype(jnp.float32)).astype(jnp.bfloat16)
    site_wide = lax.all_gather(site_tensor, "ket", axis=2, tiled=True)
    site_pairs = site_wide.reshape(rows_loc * phys, site_wide.shape[2])
    mixed_pairs = mixed.reshape(comps_loc, rows_loc * phys, cols_loc)
    panel = site_pairs
    owned = scatter_axes(
        jnp.einsum("ke,wkc->ewc", panel, mixed_pairs, preferred_element_type=jnp.float32).astype(
            jnp.bfloat16
        ),
        BRA,
        (1, 0),
        0,
    ).astype(jnp.float32)
    return jnp.transpose(owned, (1, 0, 2)).astype(jnp.bfloat16)


def solution(mesh):
    finer = Mesh(
        mesh.devices.reshape(4, 4, mesh.shape["ket"], mesh.shape["mpo"]),
        ("bra_0", "bra_1", "ket", "mpo"),
    )
    return jax.shard_map(
        local,
        mesh=finer,
        in_specs=(P("mpo", BRA, "ket"), P(BRA, None, "ket"), P(), P(), P()),
        out_specs=P("mpo", BRA, "ket"),
        check_vma=False,
    )
```

profile of v0, /device:TPU:1, one launch (start us, length us, event | category | flops | bytes accessed | tf_op | source)
XLA Modules:
  0.0 318.4 jit_solution(14838852774448430552)
XLA Ops:
  6.5 0.7 all-gather.3.cloned.1.call-update
  7.3 1.9 copy.20
  9.3 0.3 broadcast_in_dim.4
  9.6 35.1 %all_to_all.10 = bf16[8,2,192,384]{3,2,1,0:T(8,128)(2,1)S(1)} all-to-all(bf16[8,2,192,384]{3,2,1,0:T(8,128)(2,1)S(1)} %broadcast_in_dim.4), channel_id=1, replica_groups=mesh['bra_0'=4,'bra_1'=4,'ket'=8,'mpo'=2] {'ket'}, dimensions={0} | all-to-all | bytes 4718592 | tf_op jit(solution)/shard_map/all_to_all | solution.py:13
  44.7 1.4 copy.16
  46.1 0.5 copy.28
  46.6 79.0 %all-gather.3.cloned.1.call-done = bf16[3072,4,384]{2,1,0:T(4,128)(2,1)} async-done(((bf16[192,4,384]{2,1,0:T(4,128)(2,1)}), bf16[3072,4,384]{2,1,0:T(4,128)(2,1)}) %all-gather.3.cloned.1.call-update) | async-done | bytes 9437200 | tf_op jit(solution)/shard_map/all_gather | solution.py:58
  125.7 9.0 %copy.29 = bf16[384,8,4,384]{3,1,2,0:T(8,128)(2,1)} copy(bf16[384,8,4,384]{3,2,1,0:T(4,128)(2,1)} %bitcast.64) | data formatting | bytes 18874368
  134.7 6.7 %convolution_convert_fusion = bf16[384,1536]{1,0:T(8,128)(2,1)S(1)} fusion(bf16[384,3072]{1,0:T(8,128)(2,1)S(1)} %bitcast.68, bf16[3072,1536]{1,0:T(8,128)(2,1)} %bitcast.65), kind=kOutput, calls=%fused_computation.3 | convolution fusion | flops 3624468480 | bytes 12976128 | tf_op jit(solution)/shard_map/dot_general | solution.py:64
  141.4 0.3 reshape.19
  141.7 0.4 copy.17
  142.1 2.0 broadcast_in_dim.5
  144.2 4.0 %all-to-all-start.1 = ((bf16[2,2,192,4,384]{4,3,1,2,0:T(4,128)(2,1)}), bf16[2,2,192,4,384]{4,3,1,2,0:T(4,128)(2,1)S(1)}, u32[]{:S(2)}, u32[]{:S(2)}) async-start(bf16[2,2,192,4,384]{4,3,1,2,0:T(4,128)(2,1)} %broadcast_in_dim.5), calls=%async_computation.1 | async-start | bytes 4718592 | tf_op jit(solution)/shard_map/all_to_all | solution.py:13
  148.2 0.0 reduce-scatter.3.cloned.1.call-start
  148.3 0.1 fusion.8
  148.5 39.8 %all-to-all-done.1 = bf16[2,2,192,4,384]{4,3,1,2,0:T(4,128)(2,1)S(1)} async-done(((bf16[2,2,192,4,384]{4,3,1,2,0:T(4,128)(2,1)}), bf16[2,2,192,4,384]{4,3,1,2,0:T(4,128)(2,1)S(1)}, u32[]{:S(2)}, u32[]{:S(2)}) %all-to-all-start.1) | async-done | bytes 2359328 | tf_op jit(solution)/shard_map/all_to_all | solution.py:13
  188.3 0.8 copy.18
  189.1 1.6 fusion.4
  190.7 7.9 %fusion.1 = bf16[3072,2,384]{0,2,1:T(8,128)(2,1)} fusion(bf16[192,4,3072]{2,0,1:T(8,128)(2,1)} %all-gather.5.cloned.1.call-done, bf16[2,192,4,384]{3,2,0,1:T(4,128)(2,1)S(1)} %fusion.4), kind=kOutput, calls=%fused_computation.2 | convolution fusion | flops 3626237952 | bytes 10616832 | tf_op jit(solution)/shard_map/ke,wkc->ewc/dot_general | solution.py:76
  198.6 6.7 %copy.22 = bf16[3072,2,384]{2,0,1:T(8,128)(2,1)} copy(bf16[3072,2,384]{0,2,1:T(8,128)(2,1)} %fusion.1) | data formatting | bytes 9437184 | tf_op jit(solution)/shard_map/convert_element_type | solution.py:76
  205.3 5.1 %copy.23 = bf16[4,4,192,2,384]{4,2,3,1,0:T(8,128)(2,1)} copy(bf16[4,4,192,2,384]{4,2,0,1,3:T(8,128)(2,1)} %bitcast.63) | data formatting | bytes 9437184 | tf_op jit(solution)/shard_map/transpose | solution.py:30
  210.4 0.0 reduce-scatter.5.cloned.1.call-start
  210.4 65.0 %reduce-scatter.3.cloned.1.call-done = bf16[4,192,2,384]{3,1,2,0:T(8,128)(2,1)} async-done(((bf16[16,192,2,384]{3,1,2,0:T(8,128)(2,1)}), bf16[4,192,2,384]{3,1,2,0:T(8,128)(2,1)}) %reduce-scatter.3.cloned.1.call-update) | async-done | bytes 1179664 | tf_op jit(solution)/shard_map/reduce_scatter | solution.py:33
  275.4 36.5 %reduce-scatter.5.cloned.1.call-done = bf16[1,192,2,384]{3,1,2,0:T(8,128)(2,1)} async-done(((bf16[4,192,2,384]{3,1,2,0:T(8,128)(2,1)}), bf16[1,192,2,384]{3,1,2,0:T(8,128)(2,1)}) %reduce-scatter.5.cloned.1.call-update) | async-done | bytes 294928 | tf_op jit(solution)/shard_map/reduce_scatter | solution.py:33
  (16 shorter events, 0.2 us)
Async XLA Ops:
  6.5 141.7 %copy-start = (f32[12,4,4]{0,2,1:T(4,128)S(1)}, f32[12,4,4]{0,2,1:T(4,128)}, u32[]{:S(2)}) copy-start(f32[12,4,4]{0,2,1:T(4,128)} %param.7) | copy-start | bytes 2308
  6.5 2.7 copy-start.1
  6.5 119.1 %all-gather.3.cloned.1.call-start = ((), (), s32[]{:S(2)}) async-start(), calls=%async_computation.4 | async-start | bytes 10027008 | tf_op jit(solution)/shard_map/all_gather | solution.py:58
  7.3 183.4 %all-gather.5.cloned.1.call-start = ((), (), s32[]{:S(2)}) async-start(), calls=%async_computation.5 | async-start | bytes 5308416 | tf_op jit(solution)/shard_map/all_gather | solution.py:71
  144.2 4.1 %copy-start.2 = (s32[12]{0:T(128)S(1)}, s32[12]{0:T(128)}, u32[]{:S(2)}) copy-start(s32[12]{0:T(128)} %param.8) | copy-start | bytes 148
  144.2 4.1 %copy-start.3 = (s32[12]{0:T(128)S(1)}, s32[12]{0:T(128)}, u32[]{:S(2)}) copy-start(s32[12]{0:T(128)} %param.9) | copy-start | bytes 148
  144.2 44.1 %all-to-all-start.1 = ((bf16[2,2,192,4,384]{4,3,1,2,0:T(4,128)(2,1)}), bf16[2,2,192,4,384]{4,3,1,2,0:T(4,128)(2,1)S(1)}, u32[]{:S(2)}, u32[]{:S(2)}) async-start(bf16[2,2,192,4,384]{4,3,1,2,0:T(4,128)(2,1)} %broadcast_in_dim.5), calls=%async_computation.1 | async-start | bytes 4718592 | tf_op jit(solution)/shard_map/all_to_all | solution.py:13
  148.2 127.2 %reduce-scatter.3.cloned.1.call-start = ((), (), s32[]{:S(2)}) async-start(), calls=%async_computation.6 | async-start | bytes 5898240 | tf_op jit(solution)/shard_map/reduce_scatter | solution.py:33
  210.4 101.5 %reduce-scatter.5.cloned.1.call-start = ((), (), s32[]{:S(2)}) async-start(), calls=%async_computation.7 | async-start | bytes 1474560 | tf_op jit(solution)/shard_map/reduce_scatter | solution.py:33
Sparse Core Ops, SparseCore 0:
  9.1 116.5 all-gather.2
  127.5 34.0 all-gather.4
  210.5 64.8 reduce-scatter.2
  277.8 34.0 reduce-scatter.4
where the time goes:
time: 319 us; the launch traced here: 318 us
  waiting for transfers between devices  221 us (69%)
  blocking collectives  35.1 us (11%)
  local copies, waits for them, and re-layouts  28.5 us (9%)
  matrix products  16.3 us (5%)
  between operations  13.3 us (4%)
  starting transfers between devices  4.12 us (1%)
    reduce_scatter x2, waiting for transfers between devices, reduced_to_own(): blocks = lax.psum_scatter(blocks, axes[k], scatter_dimension=0, tiled=True)  101 us
    all_gather x1, waiting for transfers between devices, local(): site_full = lax.all_gather(site_tensor, BRA, axis=0, tiled=True)  79 us
    all_to_all x1, waiting for transfers between devices, from_everyone(): return lax.all_to_all(copies, axis, split_axis=0, concat_axis=0, tiled=True)  39.8 us
    all_to_all x1, blocking collectives, from_everyone(): return lax.all_to_all(copies, axis, split_axis=0, concat_axis=0, tiled=True)  35.1 us
    unnamed x11, local copies, waits for them, and re-layouts  11.4 us
    dot_general x1, matrix products, local(): jnp.einsum('ke,wkc->ewc', panel, mixed_pairs, preferred_element_type=jnp....  7.87 us
    dot_general x1, matrix products, local(): jnp.dot(piece.reshape(comps_loc * rows_loc, width), panel, preferred_elem...  6.74 us
    convert_element_type x1, local copies, waits for them, and re-layouts, local(): jnp.einsum('ke,wkc->ewc', panel, mixed_pairs, preferred_element_type=jnp....  6.73 us
  transfers between devices with their start and end apart: 5, of which 4 were waited for; matrix products, arithmetic and copies ran while one was open for 8% of the time, Pallas kernels for 0%

commit v1 on v0

--- a/solution.py
+++ b/solution.py
@@ -55,7 +55,9 @@
     hot_in = (pair_in[:, None] == comps[None, :]).astype(jnp.float32)
     mixing = jnp.einsum("pv,pw,pst->vswt", hot_out, hot_in, block_values)
     own_start = lax.axis_index("mpo") * comps_loc
-    site_full = lax.all_gather(site_tensor, BRA, axis=0, tiled=True)
+    site_full = jnp.concatenate(
+        lax.all_to_all(jnp.stack([site_tensor] * lax.axis_size(BRA)), BRA, 0, 0), axis=0
+    )
     full_rows = site_full.shape[0]
     site_flat = site_full.reshape(full_rows, phys * cols_loc)
     piece = gathered_copies(left_env, "ket", 2)

time: 319 us -> 461 us (1.45)
  waiting for transfers between devices: 221 us -> 347 us
  starting transfers between devices: 4.12 us -> 13.9 us
  local copies, waits for them, and re-layouts: 28.5 us -> 35.7 us
    all_to_all x0 -> x1, waiting for transfers between devices: none -> 167 us  [local(): lax.all_to_all(jnp.stack([site_tensor] * lax.axis_size(BRA)), BRA, 0, 0)]
    all_gather x1 -> x0, waiting for transfers between devices: 79 us -> none  [local(): site_full = lax.all_gather(site_tensor, BRA, axis=0, tiled=True)]
    reduce_scatter x2, waiting for transfers between devices: 101 us -> 151 us  [reduced_to_own(): blocks = lax.psum_scatter(blocks, axes[k], scatter_dimension=0, tiled=True)]
    all_to_all x1, waiting for transfers between devices: 39.8 us -> 28.8 us  [from_everyone(): return lax.all_to_all(copies, axis, split_axis=0, concat_axis=0, tiled=True)]
    all_to_all x0 -> x1, starting transfers between devices: none -> 8.23 us  [local(): lax.all_to_all(jnp.stack([site_tensor] * lax.axis_size(BRA)), BRA, 0, 0)]
    another operation x0 -> x1, local copies, waits for them, and re-layouts: none -> 7.29 us  [local(): jnp.stack([site_tensor] * lax.axis_size(BRA))]
  transfers between devices with their start and end apart: 5 -> 5, of which waited for: 4 -> 4; matrix products, arithmetic and copies ran while one was open for 8% -> 5% of each run, Pallas kernels for 0% -> 0%
where the time goes in v1:
time: 461 us; the launch traced here: 460 us
  waiting for transfers between devices  347 us (75%)
  local copies, waits for them, and re-layouts  35.7 us (8%)
  blocking collectives  34.9 us (8%)
  matrix products  16 us (3%)
  starting transfers between devices  13.9 us (3%)
  between operations  13.2 us (3%)
    all_to_all x1, waiting for transfers between devices, local(): lax.all_to_all(jnp.stack([site_tensor] * lax.axis_size(BRA)), BRA, 0, 0)  167 us
    reduce_scatter x2, waiting for transfers between devices, reduced_to_own(): blocks = lax.psum_scatter(blocks, axes[k], scatter_dimension=0, tiled=True)  151 us
    all_to_all x1, blocking collectives, from_everyone(): return lax.all_to_all(copies, axis, split_axis=0, concat_axis=0, tiled=True)  34.9 us
    all_to_all x1, waiting for transfers between devices, from_everyone(): return lax.all_to_all(copies, axis, split_axis=0, concat_axis=0, tiled=True)  28.8 us
    unnamed x11, local copies, waits for them, and re-layouts  10.4 us
  transfers between devices with their start and end apart: 5, of which 4 were waited for; matrix products, arithmetic and copies ran while one was open for 5% of the time, Pallas kernels for 0%

profile of v1, /device:TPU:1, one launch (start us, length us, event | category | flops | bytes accessed | tf_op | source)
XLA Modules:
  0.0 460.3 jit_solution(12973855476002474575)
XLA Ops:
  6.5 1.3 broadcast_in_dim.4
  7.8 34.9 %all_to_all.15 = bf16[8,2,192,384]{3,2,1,0:T(8,128)(2,1)S(1)} all-to-all(bf16[8,2,192,384]{3,2,1,0:T(8,128)(2,1)S(1)} %broadcast_in_dim.4), channel_id=1, replica_groups=mesh['bra_0'=4,'bra_1'=4,'ket'=8,'mpo'=2] {'ket'}, dimensions={0} | all-to-all | bytes 4718592 | tf_op jit(solution)/shard_map/all_to_all | solution.py:13
  42.7 7.3 %stack.2 = bf16[16,192,4,384]{3,2,1,0:T(4,128)(2,1)} broadcast(bf16[192,4,384]{2,1,0:T(4,128)(2,1)S(1)} %copy-done.1), dimensions={1,2,3} | broadcast | bytes 10027008 | tf_op jit(solution)/shard_map/stack | solution.py:59
  50.0 8.2 %all-to-all-start.1 = ((bf16[16,192,4,384]{3,2,1,0:T(4,128)(2,1)}), bf16[16,192,4,384]{3,2,1,0:T(4,128)(2,1)}, u32[]{:S(2)}, u32[]{:S(2)}) async-start(bf16[16,192,4,384]{3,2,1,0:T(4,128)(2,1)} %stack.2), calls=%async_computation.1 | async-start | bytes 18874368 | tf_op jit(solution)/shard_map/all_to_all | solution.py:59
  58.3 0.9 copy.20
  59.2 1.4 copy.16
  60.6 0.5 copy.28
  61.1 166.7 %all-to-all-done.1 = bf16[16,192,4,384]{3,2,1,0:T(4,128)(2,1)} async-done(((bf16[16,192,4,384]{3,2,1,0:T(4,128)(2,1)}), bf16[16,192,4,384]{3,2,1,0:T(4,128)(2,1)}, u32[]{:S(2)}, u32[]{:S(2)}) %all-to-all-start.1) | async-done | bytes 9437216 | tf_op jit(solution)/shard_map/all_to_all | solution.py:59
  227.8 9.0 %copy.29 = bf16[384,8,4,384]{3,1,2,0:T(8,128)(2,1)} copy(bf16[384,8,4,384]{3,2,1,0:T(4,128)(2,1)} %bitcast.30) | data formatting | bytes 18874368
  236.8 6.5 %convolution_convert_fusion = bf16[384,1536]{1,0:T(8,128)(2,1)S(1)} fusion(bf16[384,3072]{1,0:T(8,128)(2,1)S(1)} %bitcast.68, bf16[3072,1536]{1,0:T(8,128)(2,1)} %bitcast.65), kind=kOutput, calls=%fused_computation.3 | convolution fusion | flops 3624468480 | bytes 12976128 | tf_op jit(solution)/shard_map/dot_general | solution.py:66
  243.3 0.3 reshape.17
  243.6 0.4 copy.17
  244.0 2.0 broadcast_in_dim.5
  246.0 5.6 %all-to-all-start.2 = ((bf16[2,2,192,4,384]{4,3,1,2,0:T(4,128)(2,1)}), bf16[2,2,192,4,384]{4,3,1,2,0:T(4,128)(2,1)S(1)}, u32[]{:S(2)}, u32[]{:S(2)}) async-start(bf16[2,2,192,4,384]{4,3,1,2,0:T(4,128)(2,1)} %broadcast_in_dim.5), calls=%async_computation.2 | async-start | bytes 4718592 | tf_op jit(solution)/shard_map/all_to_all | solution.py:13
  251.6 0.1 fusion.8
  251.8 28.8 %all-to-all-done.2 = bf16[2,2,192,4,384]{4,3,1,2,0:T(4,128)(2,1)S(1)} async-done(((bf16[2,2,192,4,384]{4,3,1,2,0:T(4,128)(2,1)}), bf16[2,2,192,4,384]{4,3,1,2,0:T(4,128)(2,1)S(1)}, u32[]{:S(2)}, u32[]{:S(2)}) %all-to-all-start.2) | async-done | bytes 2359328 | tf_op jit(solution)/shard_map/all_to_all | solution.py:13
  280.6 0.8 copy.18
  281.4 1.6 fusion.4
  283.0 7.9 %fusion.1 = bf16[3072,2,384]{0,2,1:T(8,128)(2,1)} fusion(bf16[192,4,3072]{2,0,1:T(8,128)(2,1)} %all-gather.2.cloned.1.call-done, bf16[2,192,4,384]{3,2,0,1:T(4,128)(2,1)S(1)} %fusion.4), kind=kOutput, calls=%fused_computation.2 | convolution fusion | flops 3626237952 | bytes 10616832 | tf_op jit(solution)/shard_map/ke,wkc->ewc/dot_general | solution.py:78
  290.9 6.7 %copy.22 = bf16[3072,2,384]{2,0,1:T(8,128)(2,1)} copy(bf16[3072,2,384]{0,2,1:T(8,128)(2,1)} %fusion.1) | data formatting | bytes 9437184 | tf_op jit(solution)/shard_map/convert_element_type | solution.py:78
  297.6 5.1 %copy.23 = bf16[4,4,192,2,384]{4,2,3,1,0:T(8,128)(2,1)} copy(bf16[4,4,192,2,384]{4,2,0,1,3:T(8,128)(2,1)} %bitcast.64) | data formatting | bytes 9437184 | tf_op jit(solution)/shard_map/transpose | solution.py:30
  302.7 0.0 reduce-scatter.5.cloned.1.call-start
  302.7 114.4 %reduce-scatter.3.cloned.1.call-done = bf16[4,192,2,384]{3,1,2,0:T(8,128)(2,1)} async-done(((bf16[16,192,2,384]{3,1,2,0:T(8,128)(2,1)}), bf16[4,192,2,384]{3,1,2,0:T(8,128)(2,1)}) %reduce-scatter.3.cloned.1.call-update) | async-done | bytes 1179664 | tf_op jit(solution)/shard_map/reduce_scatter | solution.py:33
  417.2 36.6 %reduce-scatter.5.cloned.1.call-done = bf16[1,192,2,384]{3,1,2,0:T(8,128)(2,1)} async-done(((bf16[4,192,2,384]{3,1,2,0:T(8,128)(2,1)}), bf16[1,192,2,384]{3,1,2,0:T(8,128)(2,1)}) %reduce-scatter.5.cloned.1.call-update) | async-done | bytes 294928 | tf_op jit(solution)/shard_map/reduce_scatter | solution.py:33
  (16 shorter events, 0.2 us)
Async XLA Ops:
  6.5 245.1 %copy-start = (f32[12,4,4]{0,2,1:T(4,128)S(1)}, f32[12,4,4]{0,2,1:T(4,128)}, u32[]{:S(2)}) copy-start(f32[12,4,4]{0,2,1:T(4,128)} %param.7) | copy-start | bytes 2308
  7.8 34.9 %copy-start.1 = (bf16[192,4,384]{2,1,0:T(4,128)(2,1)S(1)}, bf16[192,4,384]{2,1,0:T(4,128)(2,1)}, u32[]{:S(2)}) copy-start(bf16[192,4,384]{2,1,0:T(4,128)(2,1)} %param.6) | copy-start | bytes 1769476
  50.0 177.8 %all-to-all-start.1 = ((bf16[16,192,4,384]{3,2,1,0:T(4,128)(2,1)}), bf16[16,192,4,384]{3,2,1,0:T(4,128)(2,1)}, u32[]{:S(2)}, u32[]{:S(2)}) async-start(bf16[16,192,4,384]{3,2,1,0:T(4,128)(2,1)} %stack.2), calls=%async_computation.1 | async-start | bytes 18874368 | tf_op jit(solution)/shard_map/all_to_all | solution.py:59
  58.2 224.8 %all-gather.2.cloned.1.call-start = ((), (), s32[]{:S(2)}) async-start(), calls=%async_computation.5 | async-start | bytes 5308416 | tf_op jit(solution)/shard_map/all_gather | solution.py:73
  246.0 5.6 %copy-start.2 = (s32[12]{0:T(128)S(1)}, s32[12]{0:T(128)}, u32[]{:S(2)}) copy-start(s32[12]{0:T(128)} %param.8) | copy-start | bytes 148
  246.0 5.6 %copy-start.3 = (s32[12]{0:T(128)S(1)}, s32[12]{0:T(128)}, u32[]{:S(2)}) copy-start(s32[12]{0:T(128)} %param.9) | copy-start | bytes 148
  246.0 34.6 %all-to-all-start.2 = ((bf16[2,2,192,4,384]{4,3,1,2,0:T(4,128)(2,1)}), bf16[2,2,192,4,384]{4,3,1,2,0:T(4,128)(2,1)S(1)}, u32[]{:S(2)}, u32[]{:S(2)}) async-start(bf16[2,2,192,4,384]{4,3,1,2,0:T(4,128)(2,1)} %broadcast_in_dim.5), calls=%async_computation.2 | async-start | bytes 4718592 | tf_op jit(solution)/shard_map/all_to_all | solution.py:13
  251.6 165.6 %reduce-scatter.3.cloned.1.call-start = ((), (), s32[]{:S(2)}) async-start(), calls=%async_computation.6 | async-start | bytes 5898240 | tf_op jit(solution)/shard_map/reduce_scatter | solution.py:33
  302.7 151.1 %reduce-scatter.5.cloned.1.call-start = ((), (), s32[]{:S(2)}) async-start(), calls=%async_computation.7 | async-start | bytes 1474560 | tf_op jit(solution)/shard_map/reduce_scatter | solution.py:33
Sparse Core Ops, SparseCore 0:
  60.9 36.3 all-gather.1
  302.8 114.3 reduce-scatter.2
  419.7 34.0 reduce-scatter.4
